TPU v7x, 128 devices: a whole 4x4x4 slice. The times are simulated.
128 devices in a mesh: dp: 8 (over y, x_hi), expert: 16 (over z, x_lo, core).
Axes of the slice: x: 4 (x_hi: 2, x_lo: 2; x = x_hi * 2 + x_lo), y: 4, z: 4, core: 2. Of those that a mesh axis runs over, the one named last changes fastest.
Arguments:
- expert_ids: int32 [4096, 8], P(('dp', 'expert')), may hold values from 0 to 15, all different within a row; in each aligned block of 32 rows (0 to 31, 32 to 63, ...) at most 20 rows name the same one
- expert_home: int32 [16], replicated, may hold values from 0 to 15, each once
- live_tokens: int32 [128], P(('dp', 'expert')), may hold values from 1 to 32, 3072 in all
- gate_weights: float32 [4096, 8], P(('dp', 'expert')), may hold values from 0.1 to 1
- output_grad: bfloat16 [4096, 7168], P(('dp', 'expert')), may hold values from -6 to 6
- saved_hidden: bfloat16 [4096, 8, 1024], P(('dp', 'expert')), may hold values from -2.5 to 2.5
- down_weight: bfloat16 [16, 1024, 7168], P('expert'), may hold values from -0.1875 to 0.1875
- dense_input: bfloat16 [4096, 7168], P(('dp', 'expert')), may hold values from -24 to 24
- latent_grad: bfloat16 [4096, 256], P(('dp', 'expert')), may hold values from -0.09375 to 0.09375
Outputs:
- hidden_grad: bfloat16 [4096, 8, 1024], P(('dp', 'expert'))
- expert_grad: float32 [16, 1024, 7168], P('expert', 'dp')
- dense_grad: float32 [7168, 256], P(('dp', 'expert'))
Inputs may be any that keep to these rules, and one draw needn't show every extreme that they name: `expert_ids`: each row names 8 different experts. Among the rows of one device no expert is named more than 20 times, and on some devices one expert is named exactly 20 times. A permutation: expert e is held at index expert_home[e] of the expert axis, in every dp replica. `live_tokens`: entry i is the number of real tokens at the start of device i, in the order of the joined dp and expert axes; the rest are padding. Some device has all 32 real.
All inputs are finite; a program needn't handle non-finite values.
Results may differ from a plain program's by a relative error of at most 0.008.
Values may be sent and summed in bfloat16 or wider, within the bound.
A program may use at most 192 MiB of HBM per device.

v0:
```python
import jax
import jax.numpy as jnp
from jax import lax
from jax.sharding import Mesh
from jax.sharding import PartitionSpec as P

DP = ("dp_0", "dp_1")
EXPERT = ("expert_0", "expert_1", "expert_2")
DP_EXPERT = ("dp_0", "dp_1", "expert_0", "expert_1", "expert_2")


def split_up(shard, dim, size):
    dims = shard.shape
    blocks = shard.reshape(*dims[:dim], size, dims[dim] // size, *dims[dim + 1 :])
    return jnp.moveaxis(blocks, dim, 0)


def in_order(blocks, dim):
    blocks = jnp.moveaxis(blocks, 0, dim)
    dims = blocks.shape
    return blocks.reshape(*dims[:dim], dims[dim] * dims[dim + 1], *dims[dim + 2 :])


def moved_by_axis(blocks, axes, sequence):
    inside = blocks.shape[1:]
    result = blocks.reshape(*(lax.axis_size(a) for a in axes), *inside)
    for k in sequence:
        result = lax.all_to_all(result, axes[k], k, k, tiled=True)
    return result.reshape(-1, *inside)


def two_step_exchange(shard, groups, sequence, split_dim, concat_dim):
    size = lax.axis_size(groups[0]) * lax.axis_size(groups[1])
    blocks = split_up(shard, split_dim, size)
    return in_order(moved_by_axis(blocks, groups, sequence), concat_dim)


def side_by_side(arrays, axis, split_dim, concat_dim, along):
    both = jnp.concatenate(arrays, axis=along)
    result, at, gathered = (
        lax.all_to_all(both, axis, split_axis=split_dim, concat_axis=concat_dim, tiled=True),
        0,
        [],
    )
    for a in arrays:
        gathered.append(lax.slice_in_dim(result, at, at + a.shape[along], axis=along))
        at += a.shape[along]
    return tuple(gathered)


def on_device(
    expert_ids,
    expert_home,
    live_tokens,
    gate_weights,
    output_grad,
    saved_hidden,
    down_weight,
    dense_input,
    latent_grad,
):
    n_group = lax.axis_size(EXPERT)
    tok_rows, top_count = expert_ids.shape
    model_width = output_grad.shape[1]
    hidden_units = saved_hidden.shape[2]
    capacity = tok_rows * top_count * 5 // (4 * n_group)
    is_live = jnp.arange(tok_rows, dtype=jnp.int32) < live_tokens[0]
    masked_grad = jnp.where(is_live[:, None], latent_grad, jnp.zeros_like(latent_grad))
    owned_columns = two_step_exchange(
        dense_input, (("dp_0", "dp_1", "expert_0", "expert_1"), "expert_2"), (1, 0), 1, 0
    )
    dense_grad = lax.dot_general(
        owned_columns,
        lax.all_gather(masked_grad, DP_EXPERT, axis=0, tiled=True),
        (((0,), (0,)), ((), ())),
        preferred_element_type=jnp.float32,
    )
    pair_count = tok_rows * top_count
    flat_ids = expert_ids.reshape(pair_count)
    expert_count = expert_home.shape[0]
    id_table = (flat_ids[:, None] == jnp.arange(expert_count, dtype=jnp.int32)[None, :]).astype(
        jnp.int32
    )
    home_slot = jnp.sum(id_table * expert_home[None, :], axis=1)
    slot_table = (home_slot[:, None] == jnp.arange(n_group, dtype=jnp.int32)[None, :]).astype(
        jnp.int32
    )
    earlier = jnp.cumsum(slot_table, axis=0) - slot_table
    position = jnp.sum(earlier * slot_table, axis=1)
    slot_index = home_slot * capacity + position
    pair_ids = jnp.arange(pair_count, dtype=jnp.int32)
    source_pair = jnp.zeros((n_group * capacity,), jnp.int32).at[slot_index].set(pair_ids)
    filled = jnp.zeros((n_group * capacity,), jnp.bool_).at[slot_index].set(True)
    source_token = source_pair // top_count
    pair_scale = (gate_weights * is_live[:, None].astype(jnp.float32)).reshape(pair_count)
    slot_scale = jnp.where(filled, pair_scale[source_pair], jnp.float32(0.0))
    grad_rows = (output_grad[source_token].astype(jnp.float32) * slot_scale[:, None]).astype(
        jnp.bfloat16
    )
    flat_hidden = saved_hidden.reshape(pair_count, hidden_units)
    hidden_rows = jnp.where(filled[:, None], flat_hidden[source_pair], jnp.zeros((), jnp.bfloat16))
    arrived_grad, arrived_hidden = side_by_side(
        (
            grad_rows.reshape(n_group, capacity, model_width),
            hidden_rows.reshape(n_group, capacity, hidden_units),
        ),
        EXPERT,
        0,
        0,
        2,
    )
    arrived_grad = arrived_grad.reshape(n_group * capacity, model_width)
    arrived_hidden = arrived_hidden.reshape(n_group * capacity, hidden_units)
    expert_weight = down_weight[0]
    input_grad = lax.dot_general(
        arrived_grad, expert_weight, (((1,), (1,)), ((), ())), preferred_element_type=jnp.float32
    ).astype(jnp.bfloat16)
    returned = two_step_exchange(
        input_grad.reshape(n_group, capacity, hidden_units),
        (("expert_0", "expert_1"), "expert_2"),
        (1, 0),
        0,
        0,
    )
    expert_grad = lax.psum_scatter(
        lax.dot_general(
            arrived_hidden,
            arrived_grad,
            (((0,), (0,)), ((), ())),
            preferred_element_type=jnp.float32,
        ),
        DP,
        scatter_dimension=0,
        tiled=True,
    )
    hidden_grad = returned.reshape(n_group * capacity, hidden_units)[slot_index].reshape(
        tok_rows, top_count, hidden_units
    )
    return (hidden_grad, expert_grad[None], dense_grad)


def solution(mesh):
    torus = Mesh(
        mesh.devices.reshape(4, 2, 4, 2, 2), ("dp_0", "dp_1", "expert_0", "expert_1", "expert_2")
    )
    in_specs = (
        P(DP_EXPERT, None),
        P(),
        P(DP_EXPERT),
        P(DP_EXPERT, None),
        P(DP_EXPERT, None),
        P(DP_EXPERT, None, None),
        P(EXPERT, None, None),
        P(DP_EXPERT, None),
        P(DP_EXPERT, None),
    )
    out_specs = (P(DP_EXPERT, None, None), P(EXPERT, DP, None), P(DP_EXPERT, None))
    return jax.shard_map(
        on_device, mesh=torus, in_specs=in_specs, out_specs=out_specs, check_vma=False
    )
```

profile of v0, /device:TPU:2, one launch (start us, length us, event | category | flops | bytes accessed | tf_op | source)
XLA Modules:
  0.0 501.7 jit_solution(9455983698504204111)
XLA Ops:
  8.0 0.8 copy.24
  8.9 0.1 eq.38
  9.0 0.7 select_reduce_fusion
  9.7 0.6 reduce-window.6
  10.3 0.2 slice_reduce_fusion
  10.5 0.1 fusion.8
  10.6 1.4 scatter_custom_fusion
  12.1 2.1 gather_fusion.2
  14.2 0.1 gather.17
  14.3 1.5 scatter_custom_fusion.1
  15.8 0.1 broadcast_in_dim.61
  15.9 6.1 %gather_fusion = bf16[320,7168]{1,0:T(8,128)(2,1)} fusion(bf16[32,7168]{1,0:T(8,128)(2,1)S(1)} %copy-done.2, s32[1024]{0:T(1024)S(1)} %get-tuple-element.6), kind=kCustom, calls=%fused_computation | custom fusion | bytes 9176320 | tf_op jit(solution)/shard_map/gather | solution.py:97
  22.1 8.1 %reshape.102 = f32[16,20,7168]{2,1,0:T(8,128)} reshape(bf16[320,7168]{1,0:T(8,128)(2,1)} %gather_fusion) | data formatting | bytes 13762560 | tf_op jit(solution)/shard_map/convert_element_type | solution.py:97
  30.9 0.1 reshape.96
  31.0 2.5 gather_fusion.1
  33.5 0.1 mul.51
  33.6 0.1 broadcast_select_fusion
  33.7 5.6 %multiply_convert_fusion = bf16[16,20,7168]{2,1,0:T(8,128)(2,1)S(1)} fusion(f32[16,20,7168]{2,1,0:T(8,128)} %reshape.102, f32[16,20]{1,0:T(8,128)S(1)} %mul.51), kind=kLoop, calls=%fused_computation.9 | loop fusion | flops 4587520 | bytes 13763840 | tf_op jit(solution)/shard_map/convert_element_type | solution.py:97
  39.3 3.3 pad_maximum_fusion
  42.7 6.9 %all-to-all-start = ((bf16[16,20,8192]{2,1,0:T(8,128)(2,1)}), bf16[16,20,8192]{2,1,0:T(8,128)(2,1)}, u32[]{:S(2)}, u32[]{:S(2)}) async-start(bf16[16,20,8192]{2,1,0:T(8,128)(2,1)} %pad_maximum_fusion), calls=%async_computation | async-start | bytes 12582912 | tf_op jit(solution)/shard_map/all_to_all | solution.py:41
  49.7 0.7 broadcast_select_fusion.1
  50.4 0.2 reduce-scatter.2.cloned.1.call-start
  50.6 70.7 %all-to-all-done = bf16[16,20,8192]{2,1,0:T(8,128)(2,1)} async-done(((bf16[16,20,8192]{2,1,0:T(8,128)(2,1)}), bf16[16,20,8192]{2,1,0:T(8,128)(2,1)}, u32[]{:S(2)}, u32[]{:S(2)}) %all-to-all-start) | async-done | bytes 5242912 | tf_op jit(solution)/shard_map/all_to_all | solution.py:41
  121.3 15.7 %convolution_bitcast_fusion = f32[1024,7168]{1,0:T(8,128)} fusion(bf16[16,20,8192]{2,1,0:T(8,128)(2,1)} %all-to-all-done), kind=kOutput, calls=%fused_computation.6 | convolution fusion | flops 4697620480 | bytes 34603008 | tf_op jit(solution)/shard_map/dot_general | solution.py:126
  137.0 1.0 copy-done.3
  138.0 2.1 reshape.100
  140.1 0.9 copy.30
  141.0 0.8 reshape.160
  141.8 4.1 all_to_all.25
  145.9 0.7 reshape.161
  146.5 1.7 copy.31
  148.2 2.6 reshape.162
  150.8 5.3 %slice.25 = bf16[16,20,7168]{2,1,0:T(8,128)(2,1)} slice(bf16[16,20,8192]{2,1,0:T(8,128)(2,1)} %all-to-all-done), slice={[0:16], [0:20], [0:7168]} | slice | bytes 9175040 | tf_op jit(solution)/shard_map/slice | solution.py:46
  156.2 7.3 %reshape.98 = bf16[320,7168]{1,0:T(8,128)(2,1)} reshape(bf16[16,20,7168]{2,1,0:T(8,128)(2,1)} %slice.25) | data formatting | bytes 9175040 | tf_op jit(solution)/shard_map/reshape | solution.py:112
  163.5 11.6 %fusion.2 = bf16[320,1024]{1,0:T(8,128)(2,1)S(1)} fusion(bf16[320,7168]{1,0:T(8,128)(2,1)} %reshape.98, bf16[1,1024,7168]{2,1,0:T(8,128)(2,1)} %param.15), kind=kOutput, calls=%fused_computation.11 | convolution fusion | flops 4697948160 | bytes 19922944 | tf_op jit(solution)/shard_map/dot_general | solution.py:115
  175.1 0.1 reshape_reshape_reshape.6
  175.2 0.4 copy.27
  175.6 4.3 all_to_all.26
  179.9 11.8 %all-to-all-start.4 = ((bf16[64,2,1792]{2,1,0:T(2,128)(2,1)}), bf16[64,2,1792]{2,1,0:T(2,128)(2,1)S(1)}, u32[]{:S(2)}, u32[]{:S(2)}) async-start(bf16[64,2,1792]{2,1,0:T(2,128)(2,1)} %reshape.162), calls=%async_computation.5 | async-start | bytes 917504 | tf_op jit(solution)/shard_map/all_to_all | solution.py:28
  191.7 1.5 copy.28
  193.2 15.3 %all-to-all-done.4 = bf16[64,2,1792]{2,1,0:T(2,128)(2,1)S(1)} async-done(((bf16[64,2,1792]{2,1,0:T(2,128)(2,1)}), bf16[64,2,1792]{2,1,0:T(2,128)(2,1)S(1)}, u32[]{:S(2)}, u32[]{:S(2)}) %all-to-all-start.4) | async-done | bytes 458784 | tf_op jit(solution)/shard_map/all_to_all | solution.py:28
  208.6 4.3 all-to-all-start.2
  212.9 1.9 reshape.163
  214.8 274.4 %all-gather.2.cloned.1.call-done = bf16[4096,256]{1,0:T(8,128)(2,1)} async-done(((bf16[32,256]{1,0:T(8,128)(2,1)}), bf16[4096,256]{1,0:T(8,128)(2,1)}) %all-gather.2.cloned.1.call-update) | async-done | bytes 2097168 | tf_op jit(solution)/shard_map/all_gather | solution.py:74
  489.2 2.7 convolution_bitcast_fusion.1
  491.9 0.2 copy.29
  492.1 0.1 reshape_reshape_reshape.7
  492.2 2.0 gather_fusion.3
  (31 shorter events, 0.3 us)
Async XLA Ops:
  8.0 4.1 copy-start
  8.0 7.9 %copy-start.2 = (bf16[32,7168]{1,0:T(8,128)(2,1)S(1)}, bf16[32,7168]{1,0:T(8,128)(2,1)}, u32[]{:S(2)}) copy-start(bf16[32,7168]{1,0:T(8,128)(2,1)} %param.13) | copy-start | bytes 1376260
  22.1 8.7 %copy-start.5 = (f32[32,8]{0,1:T(8,128)S(1)}, f32[32,8]{0,1:T(8,128)}, u32[]{:S(2)}) copy-start(f32[32,8]{0,1:T(8,128)} %param.12) | copy-start | bytes 3076
  42.7 7.0 %copy-start.4 = (bf16[32,256]{1,0:T(8,128)(2,1)S(1)}, bf16[32,256]{1,0:T(8,128)(2,1)}, u32[]{:S(2)}) copy-start(bf16[32,256]{1,0:T(8,128)(2,1)} %param.17) | copy-start | bytes 49156
  42.7 78.6 %all-to-all-start = ((bf16[16,20,8192]{2,1,0:T(8,128)(2,1)}), bf16[16,20,8192]{2,1,0:T(8,128)(2,1)}, u32[]{:S(2)}, u32[]{:S(2)}) async-start(bf16[16,20,8192]{2,1,0:T(8,128)(2,1)} %pad_maximum_fusion), calls=%async_computation | async-start | bytes 12582912 | tf_op jit(solution)/shard_map/all_to_all | solution.py:41
  49.6 439.6 %all-gather.2.cloned.1.call-start = ((), (), s32[]{:S(2)}) async-start(), calls=%async_computation.7 | async-start | bytes 2113536 | tf_op jit(solution)/shard_map/all_gather | solution.py:74
  50.4 443.8 %reduce-scatter.2.cloned.1.call-start = ((), (), s32[]{:S(2)}) async-start(), calls=%async_computation.6 | async-start | bytes 33030144 | tf_op jit(solution)/shard_map/reduce_scatter | solution.py:125
  137.0 1.0 copy-start.3
  179.9 28.7 %all-to-all-start.4 = ((bf16[64,2,1792]{2,1,0:T(2,128)(2,1)}), bf16[64,2,1792]{2,1,0:T(2,128)(2,1)S(1)}, u32[]{:S(2)}, u32[]{:S(2)}) async-start(bf16[64,2,1792]{2,1,0:T(2,128)(2,1)} %reshape.162), calls=%async_computation.5 | async-start | bytes 917504 | tf_op jit(solution)/shard_map/all_to_all | solution.py:28
  208.6 283.4 %all-to-all-start.2 = ((bf16[8,2,1,20,1024]{4,1,3,2,0:T(2,128)(2,1)}), bf16[8,2,1,20,1024]{4,1,3,2,0:T(2,128)(2,1)S(1)}, u32[]{:S(2)}, u32[]{:S(2)}) async-start(bf16[8,2,1,20,1024]{4,1,3,2,0:T(2,128)(2,1)} %copy.28), calls=%async_computation.2 | async-start | bytes 1310720 | tf_op jit(solution)/shard_map/all_to_all | solution.py:28
  212.9 281.3 %copy-start.1 = (bf16[32,8,1024]{2,1,0:T(8,128)(2,1)S(1)}, bf16[32,8,1024]{2,1,0:T(8,128)(2,1)}, u32[]{:S(2)}) copy-start(bf16[32,8,1024]{2,1,0:T(8,128)(2,1)} %param.14) | copy-start | bytes 1572868
Sparse Core Ops, SparseCore 0:
  52.7 436.4 all-gather.1
Sparse Core Ops, SparseCore 1:
  137.1 311.5 reduce-scatter.1
where the time goes:
time: 503 us; the launch traced here: 502 us
  waiting for transfers between devices  360 us (72%)
  local copies, waits for them, and re-layouts  51.8 us (10%)
  matrix products  30 us (6%)
  starting transfers between devices  23.3 us (5%)
  between operations  16.4 us (3%)
  other arithmetic  11.3 us (2%)
  blocking collectives  8.38 us (2%)
    all_gather x1, waiting for transfers between devices, on_device(): lax.all_gather(masked_grad, DP_EXPERT, axis=0, tiled=True)  274 us
    all_to_all x1, waiting for transfers between devices, side_by_side(): lax.all_to_all(both, axis, split_axis=split_dim, concat_axis=concat_dim,...  70.7 us
    all_to_all x2, starting transfers between devices, moved_by_axis(): result = lax.all_to_all(result, axes[k], k, k, tiled=True)  16.1 us
    dot_general x1, matrix products, on_device(): lax.dot_general(arrived_hidden, arrived_grad, (((0,), (0,)), ((), ())), p...  15.7 us
    all_to_all x2, waiting for transfers between devices, moved_by_axis(): result = lax.all_to_all(result, axes[k], k, k, tiled=True)  15.3 us
    dot_general x1, matrix products, on_device(): lax.dot_general(arrived_grad, expert_weight, (((1,), (1,)), ((), ())), pr...  11.6 us
  transfers between devices with their start and end apart: 5, of which 3 were waited for; matrix products, arithmetic and copies ran while one was open for 12% of the time, Pallas kernels for 0%

commit v1 on v0

--- a/solution.py
+++ b/solution.py
@@ -7,6 +7,11 @@
 DP = ("dp_0", "dp_1")
 EXPERT = ("expert_0", "expert_1", "expert_2")
 DP_EXPERT = ("dp_0", "dp_1", "expert_0", "expert_1", "expert_2")
+
+
+def gather_over(shard, axis, d):
+    repeated = jnp.stack([shard] * lax.axis_size(axis))
+    return jnp.concatenate(lax.all_to_all(repeated, axis, 0, 0), axis=d)
 
 
 def split_up(shard, dim, size):
@@ -71,7 +76,7 @@
     )
     dense_grad = lax.dot_general(
         owned_columns,
-        lax.all_gather(masked_grad, DP_EXPERT, axis=0, tiled=True),
+        gather_over(masked_grad, DP_EXPERT, 0),
         (((0,), (0,)), ((), ())),
         preferred_element_type=jnp.float32,
     )

time: 503 us -> 477 us (0.948)
  waiting for transfers between devices: 360 us -> 250 us
  blocking collectives: 8.38 us -> 86.4 us
  local copies, waits for them, and re-layouts: 51.8 us -> 58.3 us
    all_gather x1 -> x0, waiting for transfers between devices: 274 us -> none  [on_device(): lax.all_gather(masked_grad, DP_EXPERT, axis=0, tiled=True)]
    reduce_scatter x1, waiting for transfers between devices: 0.01 us -> 211 us  [on_device(): lax.psum_scatter(lax.dot_general(arrived_hidden, arrived_grad, (((0,), (0...]
    all_to_all x0 -> x1, blocking collectives: none -> 78.1 us  [side_by_side(): lax.all_to_all(both, axis, split_axis=split_dim, concat_axis=concat_dim,...]
    all_to_all x1, waiting for transfers between devices: 70.7 us -> 30.5 us  [gather_over(): return jnp.concatenate(lax.all_to_all(repeated, axis, 0, 0), axis=d)]
    all_to_all x2, waiting for transfers between devices: 15.3 us -> 8.7 us  [moved_by_axis(): result = lax.all_to_all(result, axes[k], k, k, tiled=True)]
    unnamed x17 -> x21, local copies, waits for them, and re-layouts: 7.81 us -> 12.7 us
  transfers between devices with their start and end apart: 5 -> 4, of which waited for: 3 -> 3; matrix products, arithmetic and copies ran while one was open for 12% -> 10% of each run, Pallas kernels for 0% -> 0%
where the time goes in v1:
time: 477 us; the launch traced here: 475 us
  waiting for transfers between devices  250 us (52%)
  blocking collectives  86.4 us (18%)
  local copies, waits for them, and re-layouts  58.3 us (12%)
  matrix products  28.2 us (6%)
  starting transfers between devices  23.7 us (5%)
  between operations  15 us (3%)
  other arithmetic  12.9 us (3%)
    reduce_scatter x1, waiting for transfers between devices, on_device(): lax.psum_scatter(lax.dot_general(arrived_hidden, arrived_grad, (((0,), (0...  211 us
    all_to_all x1, blocking collectives, side_by_side(): lax.all_to_all(both, axis, split_axis=split_dim, concat_axis=concat_dim,...  78.1 us
    all_to_all x1, waiting for transfers between devices, gather_over(): return jnp.concatenate(lax.all_to_all(repeated, axis, 0, 0), axis=d)  30.5 us
    all_to_all x2, starting transfers between devices, moved_by_axis(): result = lax.all_to_all(result, axes[k], k, k, tiled=True)  14.3 us
    dot_general x1, matrix products, on_device(): lax.dot_general(arrived_hidden, arrived_grad, (((0,), (0,)), ((), ())), p...  13.7 us
    unnamed x21, local copies, waits for them, and re-layouts  12.7 us
    dot_general x1, matrix products, on_device(): lax.dot_general(arrived_grad, expert_weight, (((1,), (1,)), ((), ())), pr...  12 us
  transfers between devices with their start and end apart: 4, of which 3 were waited for; matrix products, arithmetic and copies ran while one was open for 10% of the time, Pallas kernels for 0%

profile of v1, /device:TPU:2, one launch (start us, length us, event | category | flops | bytes accessed | tf_op | source)
XLA Modules:
  0.0 475.0 jit_solution(10283012527739235197)
XLA Ops:
  7.2 0.8 copy.24
  8.1 0.1 eq.38
  8.2 0.7 select_reduce_fusion
  8.9 0.6 reduce-window.6
  9.5 0.2 slice_reduce_fusion
  9.7 0.1 fusion.8
  9.8 1.4 scatter_custom_fusion
  11.3 2.1 gather_fusion.2
  13.4 0.1 gather.17
  13.5 1.5 scatter_custom_fusion.1
  15.0 0.1 broadcast_in_dim.61
  15.1 6.1 %gather_fusion = bf16[320,7168]{1,0:T(8,128)(2,1)} fusion(bf16[32,7168]{1,0:T(8,128)(2,1)S(1)} %copy-done.2, s32[1024]{0:T(1024)S(1)} %get-tuple-element.6), kind=kCustom, calls=%fused_computation | custom fusion | bytes 9176320 | tf_op jit(solution)/shard_map/gather | solution.py:102
  21.3 8.1 %reshape.108 = f32[16,20,7168]{2,1,0:T(8,128)} reshape(bf16[320,7168]{1,0:T(8,128)(2,1)} %gather_fusion) | data formatting | bytes 13762560 | tf_op jit(solution)/shard_map/convert_element_type | solution.py:102
  30.1 0.1 reshape.101
  30.2 2.5 gather_fusion.1
  32.8 0.1 broadcast_select_fusion
  32.9 8.0 %multiply_convert_fusion = bf16[16,20,7168]{2,1,0:T(8,128)(2,1)} fusion(f32[16,20,7168]{2,1,0:T(8,128)} %reshape.108, f32[16,20]{1,0:T(8,128)S(1)} %mul.51), kind=kLoop, calls=%fused_computation.9 | loop fusion | flops 4587520 | bytes 13763840 | tf_op jit(solution)/shard_map/convert_element_type | solution.py:102
  40.9 3.3 pad_maximum_fusion
  44.2 78.1 %all_to_all.30 = bf16[16,20,8192]{2,1,0:T(8,128)(2,1)S(1)} all-to-all(bf16[16,20,8192]{2,1,0:T(8,128)(2,1)S(1)} %pad_maximum_fusion), channel_id=1, replica_groups=mesh['dp_0'=4,'dp_1'=2,'expert_0'=4,'expert_1'=2,'expert_2'=2] {'expert_..., dimensions={0} | all-to-all | bytes 10485760 | tf_op jit(solution)/shard_map/all_to_all | solution.py:46
  122.2 2.6 copy-done.3
  124.9 13.7 %convolution_bitcast_fusion = f32[1024,7168]{1,0:T(8,128)} fusion(bf16[16,20,8192]{2,1,0:T(8,128)(2,1)S(1)} %all_to_all.30), kind=kOutput, calls=%fused_computation.6 | convolution fusion | flops 4697620480 | bytes 34603008 | tf_op jit(solution)/shard_map/dot_general | solution.py:131
  138.6 1.0 copy-done.5
  139.6 2.1 reshape.106
  141.7 0.9 copy.30
  142.6 0.8 reshape.166
  143.4 4.1 all_to_all.31
  147.5 0.7 reshape.167
  148.1 1.7 copy.31
  149.8 2.6 reshape.168
  152.4 8.7 %all-to-all-start.5 = ((bf16[64,2,1792]{2,1,0:T(2,128)(2,1)}), bf16[64,2,1792]{2,1,0:T(2,128)(2,1)S(1)}, u32[]{:S(2)}, u32[]{:S(2)}) async-start(bf16[64,2,1792]{2,1,0:T(2,128)(2,1)} %reshape.168), calls=%async_computation.6 | async-start | bytes 917504 | tf_op jit(solution)/shard_map/all_to_all | solution.py:33
  161.2 5.4 %slice.25 = bf16[16,20,7168]{2,1,0:T(8,128)(2,1)} slice(bf16[16,20,8192]{2,1,0:T(8,128)(2,1)} %copy-done.3), slice={[0:16], [0:20], [0:7168]} | slice | bytes 9175040 | tf_op jit(solution)/shard_map/slice | solution.py:51
  166.6 7.3 %reshape.103 = bf16[320,7168]{1,0:T(8,128)(2,1)} reshape(bf16[16,20,7168]{2,1,0:T(8,128)(2,1)} %slice.25) | data formatting | bytes 9175040 | tf_op jit(solution)/shard_map/reshape | solution.py:117
  174.0 12.0 %fusion.2 = bf16[320,1024]{1,0:T(8,128)(2,1)S(1)} fusion(bf16[320,7168]{1,0:T(8,128)(2,1)} %reshape.103, bf16[1,1024,7168]{2,1,0:T(8,128)(2,1)} %param.15), kind=kOutput, calls=%fused_computation.11 | convolution fusion | flops 4697948160 | bytes 19922944 | tf_op jit(solution)/shard_map/dot_general | solution.py:120
  186.0 0.1 reshape_reshape_reshape.6
  186.2 0.4 copy.27
  186.5 4.3 all_to_all.32
  190.8 1.6 stack.2
  192.4 9.4 %all-to-all-start.3 = ((bf16[128,32,256]{2,1,0:T(8,128)(2,1)}), bf16[128,32,256]{2,1,0:T(8,128)(2,1)S(1)}, u32[]{:S(2)}, u32[]{:S(2)}) async-start(bf16[128,32,256]{2,1,0:T(8,128)(2,1)} %stack.2), calls=%async_computation.4 | async-start | bytes 4194304 | tf_op jit(solution)/shard_map/all_to_all | solution.py:14
  201.8 1.5 copy.28
  203.3 30.5 %all-to-all-done.3 = bf16[128,32,256]{2,1,0:T(8,128)(2,1)S(1)} async-done(((bf16[128,32,256]{2,1,0:T(8,128)(2,1)}), bf16[128,32,256]{2,1,0:T(8,128)(2,1)S(1)}, u32[]{:S(2)}, u32[]{:S(2)}) %all-to-all-start.3) | async-done | bytes 2097184 | tf_op jit(solution)/shard_map/all_to_all | solution.py:14
  233.8 5.6 %all-to-all-start.2 = ((bf16[8,2,1,20,1024]{4,1,3,2,0:T(2,128)(2,1)}), bf16[8,2,1,20,1024]{4,1,3,2,0:T(2,128)(2,1)S(1)}, u32[]{:S(2)}, u32[]{:S(2)}) async-start(bf16[8,2,1,20,1024]{4,1,3,2,0:T(2,128)(2,1)} %copy.28), calls=%async_computation.2 | async-start | bytes 1310720 | tf_op jit(solution)/shard_map/all_to_all | solution.py:33
  239.4 4.1 reshape.169
  243.5 2.4 convolution_bitcast_fusion.1
  246.0 8.7 %all-to-all-done.2 = bf16[8,2,1,20,1024]{4,1,3,2,0:T(2,128)(2,1)S(1)} async-done(((bf16[8,2,1,20,1024]{4,1,3,2,0:T(2,128)(2,1)}), bf16[8,2,1,20,1024]{4,1,3,2,0:T(2,128)(2,1)S(1)}, u32[]{:S(2)}, u32[]{:S(2)}) %all-to-all-start.2) | async-done | bytes 655392 | tf_op jit(solution)/shard_map/all_to_all | solution.py:33
  254.7 0.2 copy.29
  254.8 0.1 reshape_reshape_reshape.7
  255.0 2.0 gather_fusion.3
  256.9 211.2 %reduce-scatter.2.cloned.1.call-done = f32[128,7168]{1,0:T(8,128)} async-done(((f32[1024,7168]{1,0:T(8,128)}), f32[128,7168]{1,0:T(8,128)}) %reduce-scatter.2.cloned.1.call-update) | async-done | bytes 3670032 | tf_op jit(solution)/shard_map/reduce_scatter | solution.py:130
  (33 shorter events, 0.4 us)
Async XLA Ops:
  7.2 4.1 copy-start
  7.2 8.0 %copy-start.2 = (bf16[32,7168]{1,0:T(8,128)(2,1)S(1)}, bf16[32,7168]{1,0:T(8,128)(2,1)}, u32[]{:S(2)}) copy-start(bf16[32,7168]{1,0:T(8,128)(2,1)} %param.13) | copy-start | bytes 1376260
  7.2 461.0 %reduce-scatter.2.cloned.1.call-start = ((), (), s32[]{:S(2)}) async-start(), calls=%async_computation.7 | async-start | bytes 33030144 | tf_op jit(solution)/shard_map/reduce_scatter | solution.py:130
  21.3 8.7 %copy-start.7 = (f32[32,8]{0,1:T(8,128)S(1)}, f32[32,8]{0,1:T(8,128)}, u32[]{:S(2)}) copy-start(f32[32,8]{0,1:T(8,128)} %param.12) | copy-start | bytes 3076
  122.2 2.6 copy-start.3
  138.6 1.0 copy-start.5
  139.6 21.6 %copy-start.6 = (bf16[32,256]{1,0:T(8,128)(2,1)S(1)}, bf16[32,256]{1,0:T(8,128)(2,1)}, u32[]{:S(2)}) copy-start(bf16[32,256]{1,0:T(8,128)(2,1)} %param.17) | copy-start | bytes 49156
  152.4 34.1 %all-to-all-start.5 = ((bf16[64,2,1792]{2,1,0:T(2,128)(2,1)}), bf16[64,2,1792]{2,1,0:T(2,128)(2,1)S(1)}, u32[]{:S(2)}, u32[]{:S(2)}) async-start(bf16[64,2,1792]{2,1,0:T(2,128)(2,1)} %reshape.168), calls=%async_computation.6 | async-start | bytes 917504 | tf_op jit(solution)/shard_map/all_to_all | solution.py:33
  186.5 47.3 %copy-start.4 = (bf16[64,2,1792]{2,1,0:T(2,128)(2,1)}, bf16[64,2,1792]{2,1,0:T(2,128)(2,1)S(1)}, u32[]{:S(2)}) copy-start(bf16[64,2,1792]{2,1,0:T(2,128)(2,1)S(1)} %all-to-all-done.5) | copy-start | bytes 1376260
  192.4 41.4 %all-to-all-start.3 = ((bf16[128,32,256]{2,1,0:T(8,128)(2,1)}), bf16[128,32,256]{2,1,0:T(8,128)(2,1)S(1)}, u32[]{:S(2)}, u32[]{:S(2)}) async-start(bf16[128,32,256]{2,1,0:T(8,128)(2,1)} %stack.2), calls=%async_computation.4 | async-start | bytes 4194304 | tf_op jit(solution)/shard_map/all_to_all | solution.py:14
  233.8 20.8 %all-to-all-start.2 = ((bf16[8,2,1,20,1024]{4,1,3,2,0:T(2,128)(2,1)}), bf16[8,2,1,20,1024]{4,1,3,2,0:T(2,128)(2,1)S(1)}, u32[]{:S(2)}, u32[]{:S(2)}) async-start(bf16[8,2,1,20,1024]{4,1,3,2,0:T(2,128)(2,1)} %copy.28), calls=%async_computation.2 | async-start | bytes 1310720 | tf_op jit(solution)/shard_map/all_to_all | solution.py:33
  239.4 228.7 %copy-start.1 = (bf16[32,8,1024]{2,1,0:T(8,128)(2,1)S(1)}, bf16[32,8,1024]{2,1,0:T(8,128)(2,1)}, u32[]{:S(2)}) copy-start(bf16[32,8,1024]{2,1,0:T(8,128)(2,1)} %param.14) | copy-start | bytes 1572868
Sparse Core Ops, SparseCore 0:
  138.7 329.3 reduce-scatter.1
